TPU v7x, 32 devices: a whole 2x2x4 slice. The times are simulated.
32 devices in a mesh: src: 8 (over z, x), tgt: 4 (over y, core).
Axes of the slice: x: 2, y: 2, z: 4, core: 2. Of those that a mesh axis runs over, the one named last changes fastest.
Arguments:
- sources: bfloat16 [65536, 64], P(('src', 'tgt')), may hold values from -2.09375 to 2.09375
- targets: bfloat16 [65536, 64], P('tgt'), may hold values from -2.09375 to 2.09375
- potential: float32 [65536], P('src'), may hold values from -1 to 112
- block_map: int32 [256, 20], P('src'), may hold values from -1 to 255, as said below
- counts: int32 [256], P('src'), may hold values from 10 to 20, as said below
- step_history: float32 [8, 65536], P(None, ('src', 'tgt')), may hold values from -13 to 13
- slope_history: float32 [8, 65536], P(None, ('src', 'tgt')), may hold values from -64 to 64, as said below
Outputs:
- gradient: float32 [65536], P(('src', 'tgt'))
- direction: float32 [65536], P(('src', 'tgt'))
- target_potential: float32 [65536], P('tgt')
Inputs may be any that keep to these rules, and one draw needn't show every extreme that they name: `block_map`: row b lists counts[b] different target block numbers in slots 0 to counts[b] - 1 and -1 in the other slots; every target block is listed in some row. `counts`: some source block lists exactly 20 target blocks in every draw. For every k the sum over all points of step_history[k] slope_history[k] is positive.
All inputs are finite; a program needn't handle non-finite values.
Results may differ from a plain program's by a relative error of at most 0.0008.
Values may be sent and summed in bfloat16 or wider, within the bound.
A program may use at most 64 MiB of HBM per device.

v0:
```python
import jax
import jax.numpy as jnp
from jax import lax
from jax.sharding import PartitionSpec as P

BLOCK = 256
entropy = 0.5
tile_group = 16


def merged(part, axis, combine):
    gathered = jax.tree.map(lambda a: lax.all_gather(a, axis), part)

    def take(source):
        return jax.tree.map(lambda a: lax.dynamic_index_in_dim(a, source, 0, False), gathered)

    return lax.fori_loop(
        1, lax.axis_size(axis), lambda source, state: combine(state, take(source)), take(0)
    )


def combine_columns(earlier, later):
    peak = jnp.maximum(earlier[0], later[0])
    return (peak, earlier[1] * jnp.exp(earlier[0] - peak) + later[1] * jnp.exp(later[0] - peak))


def pair_scores(source_tiles, potential_tiles, target_tiles, source_ids, target_ids):
    rows_in = source_tiles[source_ids]
    columns_in = target_tiles[target_ids]
    product = jnp.einsum("gid,gjd->gij", rows_in, columns_in, preferred_element_type=jnp.float32)
    return (potential_tiles[source_ids][:, :, None] + product) / entropy


def upper_solve(upper, right_side, stored):
    values = [None] * stored
    for row in reversed(range(stored)):
        accum = right_side[row]
        for other in range(row + 1, stored):
            accum = accum - upper[row, other] * values[other]
        values[row] = accum / upper[row, row]
    return jnp.stack(values)


def lower_solve(upper, right_side, stored):
    values = [None] * stored
    for row in range(stored):
        accum = right_side[row]
        for other in range(row):
            accum = accum - upper[other, row] * values[other]
        values[row] = accum / upper[row, row]
    return jnp.stack(values)


def per_device(sources, targets, potential, block_map, counts, step_history, slope_history):
    gathered = lax.all_gather(sources, "tgt", axis=0, tiled=True)
    features = gathered.shape[1]
    source_blocks = gathered.shape[0] // BLOCK
    target_blocks = targets.shape[0] // BLOCK
    listed = block_map.shape[1]
    source_tiles = gathered.reshape(source_blocks, BLOCK, features)
    target_tiles = targets.reshape(target_blocks, BLOCK, features)
    potential_tiles = potential.reshape(source_blocks, BLOCK)
    column_rank = lax.axis_index("tgt")
    slot_index = jnp.arange(listed, dtype=jnp.int32)
    owned = (slot_index[None, :] < counts[:, None]) & (block_map // target_blocks == column_rank)
    flat_owned = owned.reshape(-1)
    slot_total = source_blocks * listed
    padded_total = -(-slot_total // tile_group) * tile_group
    flat_index = jnp.arange(slot_total, dtype=jnp.int32)
    ordering = jnp.argsort(jnp.where(flat_owned, 0, slot_total) + flat_index)
    ordering = jnp.concatenate([ordering, jnp.zeros((padded_total - slot_total,), jnp.int32)])
    pair_total = jnp.sum(flat_owned.astype(jnp.int32))
    live_pairs = jnp.arange(padded_total, dtype=jnp.int32) < pair_total
    source_list = jnp.where(live_pairs, ordering // listed, 0)
    target_list = jnp.where(
        live_pairs, block_map.reshape(-1)[ordering] - column_rank * target_blocks, target_blocks
    )
    turn_count = (pair_total + tile_group - 1) // tile_group

    def group_of(turn_index):
        offset = turn_index * tile_group
        source_ids = lax.dynamic_slice_in_dim(source_list, offset, tile_group)
        target_ids = lax.dynamic_slice_in_dim(target_list, offset, tile_group)
        live = lax.dynamic_slice_in_dim(live_pairs, offset, tile_group)
        clipped = jnp.minimum(target_ids, target_blocks - 1)
        scores = pair_scores(source_tiles, potential_tiles, target_tiles, source_ids, clipped)
        return (scores, source_ids, target_ids, clipped, live)

    def column_turn(turn_index, carry):
        peak, total = carry
        scores, source_ids, target_ids, clipped, live = group_of(turn_index)
        tile_peak = jnp.max(scores, axis=1)
        tile_total = jnp.sum(jnp.exp(scores - tile_peak[:, None, :]), axis=1)
        new_peak = peak.at[target_ids].max(tile_peak)
        total = total * jnp.exp(peak - new_peak)
        total = total.at[target_ids].add(tile_total * jnp.exp(tile_peak - new_peak[target_ids]))
        return (new_peak, total)

    start_peak = jnp.full((target_blocks + 1, BLOCK), -1e30, jnp.float32)
    start_total = jnp.zeros((target_blocks + 1, BLOCK), jnp.float32)
    peak, total = lax.fori_loop(0, turn_count, column_turn, (start_peak, start_total))
    local_peak = peak[:target_blocks].reshape(-1)
    local_total = total[:target_blocks].reshape(-1)
    merged_peak, merged_total = merged((local_peak, local_total), "src", combine_columns)
    logs = merged_peak + jnp.log(merged_total)
    target_potential = -entropy * logs
    log_tiles = logs.reshape(target_blocks, BLOCK)

    def row_turn(turn_index, masses):
        scores, source_ids, target_ids, clipped, live = group_of(turn_index)
        weights = jnp.exp(scores - log_tiles[clipped][:, None, :])
        row_sums = jnp.where(live[:, None], jnp.sum(weights, axis=2), 0.0)
        return masses.at[source_ids].add(row_sums)

    masses = lax.fori_loop(0, turn_count, row_turn, jnp.zeros((source_blocks, BLOCK), jnp.float32))
    row_total = lax.psum_scatter(masses.reshape(-1), "tgt", scatter_dimension=0, tiled=True)
    ratio = source_blocks * lax.axis_size("src") / (target_blocks * lax.axis_size("tgt"))
    gradient = 1.0 - ratio * row_total
    stored = step_history.shape[0]
    highest = lax.Precision.HIGHEST
    cross_local = jnp.dot(step_history, slope_history.T, precision=highest)
    slope_local = jnp.dot(slope_history, slope_history.T, precision=highest)
    step_grad = jnp.dot(step_history, gradient, precision=highest)
    slope_grad = jnp.dot(slope_history, gradient, precision=highest)
    cross, slopes, step_dots, slope_dots = lax.psum(
        (cross_local, slope_local, step_grad, slope_grad), ("src", "tgt")
    )
    diagonal = jnp.diag(cross)
    scale = cross[stored - 1, stored - 1] / slopes[stored - 1, stored - 1]
    first_solve = upper_solve(cross, step_dots, stored)
    right_side = (
        diagonal * first_solve
        + scale * jnp.dot(slopes, first_solve, precision=highest)
        - scale * slope_dots
    )
    second_solve = lower_solve(cross, right_side, stored)
    result = (
        scale * gradient
        + jnp.dot(second_solve, step_history, precision=highest)
        - scale * jnp.dot(first_solve, slope_history, precision=highest)
    )
    direction = -result
    return (gradient, direction, target_potential)


def solution(mesh):
    in_specs = (
        P(("src", "tgt"), None),
        P("tgt", None),
        P("src"),
        P("src", None),
        P("src"),
        P(None, ("src", "tgt")),
        P(None, ("src", "tgt")),
    )
    out_specs = (P(("src", "tgt")), P(("src", "tgt")), P("tgt"))
    return jax.shard_map(
        per_device, mesh=mesh, in_specs=in_specs, out_specs=out_specs, check_vma=False
    )
```

profile of v0, /device:TPU:0, one launch (start us, length us, event | category | flops | bytes accessed | tf_op | source)
XLA Modules:
  0.0 390.4 jit_solution(8471207344332975932)
XLA Ops:
  11.1 4.8 %copy.31 = bf16[16384,64]{1,0:T(8,128)(2,1)} copy(bf16[16384,64]{0,1:T(8,128)(2,1)} %param.14) | data formatting | bytes 4194304 | tf_op args[1]
  15.9 4.4 %sort.17 = (s32[640]{0:T(1024)}, s32[640]{0:T(1024)S(1)}) sort(s32[640]{0:T(1024)S(1)} %iota_add_fusion, s32[640]{0:T(1024)S(1)} %iota.27), dimensions={0}, to_apply=%region_1.2 | sort | flops 6400 | bytes 10240 | tf_op jit(solution)/shard_map/jit(argsort)/sort | solution.py:70
  21.0 2.8 gather_fusion.7
  26.8 3.8 all-gather.4.cloned.1.call-done
  32.7 84.1 %while.39 = (s32[]{:T(128)}, f32[65,256]{1,0:T(8,128)S(1)}, f32[65,256]{1,0:T(8,128)S(1)}, s32[]{:T(128)}, s32[640]{0:T(1024)S(1)}, /*index=5*/s32[640]{0:T(1024...) while((s32[]{:T(128)}, f32[65,256]{1,0:T(8,128)S(1)}, ...), condition=%wide.region_7.8_spmd, body=%wide.region_2.7_spmd.sunk | while | flops 141602464 | bytes 20809704 | solution.py:101
  34.2 2.9 gather_fusion.2
  42.6 2.9 gather_fusion.2
  51.0 2.9 gather_fusion.2
  59.4 2.9 gather_fusion.2
  67.8 2.9 gather_fusion.2
  76.2 2.9 gather_fusion.2
  84.6 2.9 gather_fusion.2
  93.0 2.9 gather_fusion.2
  101.4 2.9 gather_fusion.2
  109.9 2.9 gather_fusion.2
  116.9 31.7 %all-gather = f32[8,1,16384]{2,1,0:T(1,128)S(1)} all-gather(f32[1,1,16384]{2,1,0:T(1,128)S(1)} %reshape.154), channel_id=1, replica_groups=mesh['src'=8,'tgt'=4] {'src'}, dimensions={0}, use_global_device_ids=true | all-gather | bytes 589824 | tf_op jit(solution)/shard_map/all_gather | solution.py:12
  149.0 31.7 %all-gather.1 = f32[8,1,16384]{2,1,0:T(1,128)S(1)} all-gather(f32[1,1,16384]{2,1,0:T(1,128)S(1)} %reshape.156), channel_id=1, replica_groups=mesh['src'=8,'tgt'=4] {'src'}, dimensions={0}, use_global_device_ids=true | all-gather | bytes 589824 | tf_op jit(solution)/shard_map/all_gather | solution.py:12
  183.1 90.2 %while.41 = (s32[]{:T(128)}, f32[32,256]{1,0:T(8,128)S(1)}, s32[]{:T(128)}, s32[640]{0:T(1024)S(1)}, pred[640]{0:T(1024)(128)(4,1)S(1)}, /*index=5*/f32[32,256]{...) while((s32[]{:T(128)}, f32[32,256]{1,0:T(8,128)S(1)}, ...), condition=%wide.region_13.14_spmd, body=%wide.region_10.13_spmd.sunk | while | flops 138418288 | bytes 3319143 | solution.py:115
  184.6 3.8 gather_fusion.4
  189.0 2.3 exponential_reduce_fusion.5
  193.6 3.8 gather_fusion.4
  198.0 2.3 exponential_reduce_fusion.5
  202.6 3.8 gather_fusion.4
  211.6 3.8 gather_fusion.4
  220.6 3.8 gather_fusion.4
  229.7 3.8 gather_fusion.4
  238.7 3.8 gather_fusion.4
  247.7 3.8 gather_fusion.4
  256.7 3.8 gather_fusion.4
  265.7 3.8 gather_fusion.4
  273.3 10.3 %all-reduce = f32[8192]{0:T(1024)S(1)} all-reduce(f32[8192]{0:T(1024)S(1)} %bitcast.147), channel_id=2, replica_groups=mesh['src'=8,'tgt'=4] {'tgt'}, use_global_device_ids=true, to_apply=%region_14.15.clone | all-reduce | flops 8192 | bytes 65536
  284.2 37.0 %all-reduce.1 = (f32[8]{0:T(128)S(1)}, f32[8,8]{1,0:T(8,128)S(1)}, f32[8,8]{1,0:T(8,128)S(1)}, f32[8]{0:T(128)S(1)}) all-reduce(f32[8]{0:T(128)S(1)} %convolution_bitcast_fusion.2, f32[8,8]{1,0:T(8,128)S(1)} %fusion.29, f32[8,8]{1,0:T(8,128)S(1)} %fusion.30, ...), channel_id=1, replica_groups=mesh['src'=8,'tgt'=4] {'src','tgt'}, use_global_device_ids=true, to_apply=%region_17.18 | all-reduce | flops 144 | bytes 1152 | tf_op jit(solution)/shard_map/psum | solution.py:125
  (332 shorter events, 117.9 us)
Async XLA Ops:
  7.2 19.2 %copy-start = (f32[8,2048]{1,0:T(8,128)S(1)}, f32[8,2048]{1,0:T(8,128)}, u32[]{:S(2)}) copy-start(f32[8,2048]{1,0:T(8,128)} %param.19) | copy-start | bytes 196612
  7.2 8.7 %copy-start.5 = (f32[8192]{0:T(1024)S(1)}, f32[8192]{0:T(1024)}, u32[]{:S(2)}) copy-start(f32[8192]{0:T(1024)} %param.15) | copy-start | bytes 98308
  7.2 23.4 %all-gather.4.cloned.1.call-start = ((), (), s32[]{:S(2)}) async-start(), calls=%async_computation | async-start | bytes 1310720 | tf_op jit(solution)/shard_map/all_gather | solution.py:55
  11.0 12.8 %copy-start.6 = (u32[32]{0:T(128)S(1)}, u32[32]{0:T(128)}, u32[]{:S(2)}) copy-start(u32[32]{0:T(128)} %constant.169) | copy-start | bytes 388
  11.0 15.5 %copy-start.3 = (f32[8,2048]{1,0:T(8,128)S(1)}, f32[8,2048]{1,0:T(8,128)}, u32[]{:S(2)}) copy-start(f32[8,2048]{1,0:T(8,128)} %param.18) | copy-start | bytes 196612
  32.7 1.5 copy-start.1
  38.5 2.6 copy-start.2
  41.1 1.5 copy-start.1
  46.9 2.6 copy-start.2
  49.5 1.5 copy-start.1
  55.3 2.6 copy-start.2
  57.9 1.5 copy-start.1
  63.7 2.6 copy-start.2
  66.3 1.5 copy-start.1
  72.1 2.6 copy-start.2
  74.7 1.5 copy-start.1
  80.5 2.6 copy-start.2
  83.2 1.5 copy-start.1
  88.9 2.6 copy-start.2
  91.6 1.5 copy-start.1
  97.3 2.6 copy-start.2
  100.0 1.5 copy-start.1
  105.7 2.6 copy-start.2
  108.4 1.5 copy-start.1
  114.2 2.6 copy-start.2
  283.6 100.0 %copy-start.4 = (f32[2048]{0:T(1024)}, f32[2048]{0:T(1024)S(1)}, u32[]{:S(2)}) copy-start(f32[2048]{0:T(1024)S(1)} %dynamic-slice_subtract_fusion) | copy-start | bytes 24580
Sparse Core Ops, SparseCore 0:
  9.6 21.0 all-gather.3
where the time goes:
time: 393 us; the launch traced here: 390 us
  local copies, waits for them, and re-layouts  118 us (30%)
  blocking collectives  111 us (28%)
  between operations  72.7 us (18%)
  other arithmetic  44.5 us (11%)
  matrix products  37.6 us (10%)
  waiting for transfers between devices  4.5 us (1%)
    gather x20, local copies, waits for them, and re-layouts, pair_scores(): columns_in = target_tiles[target_ids]  67.8 us
    all_gather x2, blocking collectives, merged(): gathered = jax.tree.map(lambda a: lax.all_gather(a, axis), part)  63.4 us
    psum x1, blocking collectives, per_device(): lax.psum((cross_local, slope_local, step_grad, slope_grad), ('src', 'tgt'))  37 us
    dot_general x20, matrix products, pair_scores(): jnp.einsum('gid,gjd->gij', rows_in, columns_in, preferred_element_type=jn...  36.1 us
    gather x20, local copies, waits for them, and re-layouts, pair_scores(): rows_in = source_tiles[source_ids]  15 us
    gather x20, local copies, waits for them, and re-layouts, pair_scores(): return (potential_tiles[source_ids][:, :, None] + product) / entropy  11.5 us
    reduce_sum x10, other arithmetic, column_turn(): tile_total = jnp.sum(jnp.exp(scores - tile_peak[:, None, :]), axis=1)  10.8 us
    unnamed x1, blocking collectives  10.3 us
  transfers between devices with their start and end apart: 1, of which 1 were waited for; matrix products, arithmetic and copies ran while one was open for 4% of the time, Pallas kernels for 0%

commit v1 on v0

--- a/solution.py
+++ b/solution.py
@@ -6,6 +6,11 @@
 BLOCK = 256
 entropy = 0.5
 tile_group = 16
+
+
+def one_after_other(x, first, second):
+    half = lax.psum(x, first)
+    return lax.psum(half, second)
 
 
 def merged(part, axis, combine):
@@ -122,8 +127,8 @@
     slope_local = jnp.dot(slope_history, slope_history.T, precision=highest)
     step_grad = jnp.dot(step_history, gradient, precision=highest)
     slope_grad = jnp.dot(slope_history, gradient, precision=highest)
-    cross, slopes, step_dots, slope_dots = lax.psum(
-        (cross_local, slope_local, step_grad, slope_grad), ("src", "tgt")
+    cross, slopes, step_dots, slope_dots = one_after_other(
+        (cross_local, slope_local, step_grad, slope_grad), "tgt", "src"
     )
     diagonal = jnp.diag(cross)
     scale = cross[stored - 1, stored - 1] / slopes[stored - 1, stored - 1]

time: 393 us -> 379 us (0.964)
  blocking collectives: 111 us -> 97.3 us
    psum x1 -> x2, blocking collectives: 37 us -> 23.6 us  [the longest x1 17.6 us: one_after_other(): return lax.psum(half, second)]
  transfers between devices with their start and end apart: 1 -> 1, of which waited for: 1 -> 1; matrix products, arithmetic and copies ran while one was open for 4% -> 5% of each run, Pallas kernels for 0% -> 0%
where the time goes in v1:
time: 379 us; the launch traced here: 377 us
  local copies, waits for them, and re-layouts  118 us (31%)
  blocking collectives  97.3 us (26%)
  between operations  72.7 us (19%)
  other arithmetic  44.5 us (12%)
  matrix products  37.6 us (10%)
  waiting for transfers between devices  4.5 us (1%)
    gather x20, local copies, waits for them, and re-layouts, pair_scores(): columns_in = target_tiles[target_ids]  67.8 us
    all_gather x2, blocking collectives, merged(): gathered = jax.tree.map(lambda a: lax.all_gather(a, axis), part)  63.4 us
    dot_general x20, matrix products, pair_scores(): jnp.einsum('gid,gjd->gij', rows_in, columns_in, preferred_element_type=jn...  36.1 us
    psum x1, blocking collectives, one_after_other(): return lax.psum(half, second)  17.6 us
    gather x20, local copies, waits for them, and re-layouts, pair_scores(): rows_in = source_tiles[source_ids]  15 us
    gather x20, local copies, waits for them, and re-layouts, pair_scores(): return (potential_tiles[source_ids][:, :, None] + product) / entropy  11.5 us
    reduce_sum x10, other arithmetic, column_turn(): tile_total = jnp.sum(jnp.exp(scores - tile_peak[:, None, :]), axis=1)  10.8 us
    unnamed x1, blocking collectives  10.3 us
  transfers between devices with their start and end apart: 1, of which 1 were waited for; matrix products, arithmetic and copies ran while one was open for 5% of the time, Pallas kernels for 0%

profile of v1, /device:TPU:0, one launch (start us, length us, event | category | flops | bytes accessed | tf_op | source)
XLA Modules:
  0.0 377.1 jit_solution(15358700447379526323)
XLA Ops:
  11.1 4.8 %copy.31 = bf16[16384,64]{1,0:T(8,128)(2,1)} copy(bf16[16384,64]{0,1:T(8,128)(2,1)} %param.14) | data formatting | bytes 4194304 | tf_op args[1]
  15.9 4.4 %sort.17 = (s32[640]{0:T(1024)}, s32[640]{0:T(1024)S(1)}) sort(s32[640]{0:T(1024)S(1)} %iota_add_fusion, s32[640]{0:T(1024)S(1)} %iota.27), dimensions={0}, to_apply=%region_1.2 | sort | flops 6400 | bytes 10240 | tf_op jit(solution)/shard_map/jit(argsort)/sort | solution.py:75
  21.0 2.8 gather_fusion.7
  26.8 3.8 %all-gather.4.cloned.1.call-done = bf16[8192,64]{0,1:T(8,128)(2,1)} async-done(((bf16[2048,64]{0,1:T(8,128)(2,1)}), bf16[8192,64]{0,1:T(8,128)(2,1)}) %all-gather.4.cloned.1.call-update) | async-done | bytes 1048592 | tf_op jit(solution)/shard_map/all_gather | solution.py:60
  32.7 84.1 %while.39 = (s32[]{:T(128)}, f32[65,256]{1,0:T(8,128)S(1)}, f32[65,256]{1,0:T(8,128)S(1)}, s32[]{:T(128)}, s32[640]{0:T(1024)S(1)}, /*index=5*/s32[640]{0:T(1024...) while((s32[]{:T(128)}, f32[65,256]{1,0:T(8,128)S(1)}, ...), condition=%wide.region_7.8_spmd, body=%wide.region_2.7_spmd.sunk | while | flops 141602464 | bytes 20809704 | solution.py:106
  34.2 2.9 gather_fusion.2
  42.6 2.9 gather_fusion.2
  51.0 2.9 gather_fusion.2
  59.4 2.9 gather_fusion.2
  67.8 2.9 gather_fusion.2
  76.2 2.9 gather_fusion.2
  84.6 2.9 gather_fusion.2
  93.0 2.9 gather_fusion.2
  101.4 2.9 gather_fusion.2
  109.9 2.9 gather_fusion.2
  116.9 31.7 %all-gather = f32[8,1,16384]{2,1,0:T(1,128)S(1)} all-gather(f32[1,1,16384]{2,1,0:T(1,128)S(1)} %reshape.154), channel_id=1, replica_groups=mesh['src'=8,'tgt'=4] {'src'}, dimensions={0}, use_global_device_ids=true | all-gather | bytes 589824 | tf_op jit(solution)/shard_map/all_gather | solution.py:17
  149.0 31.7 %all-gather.1 = f32[8,1,16384]{2,1,0:T(1,128)S(1)} all-gather(f32[1,1,16384]{2,1,0:T(1,128)S(1)} %reshape.156), channel_id=1, replica_groups=mesh['src'=8,'tgt'=4] {'src'}, dimensions={0}, use_global_device_ids=true | all-gather | bytes 589824 | tf_op jit(solution)/shard_map/all_gather | solution.py:17
  183.1 90.2 %while.41 = (s32[]{:T(128)}, f32[32,256]{1,0:T(8,128)S(1)}, s32[]{:T(128)}, s32[640]{0:T(1024)S(1)}, pred[640]{0:T(1024)(128)(4,1)S(1)}, /*index=5*/f32[32,256]{...) while((s32[]{:T(128)}, f32[32,256]{1,0:T(8,128)S(1)}, ...), condition=%wide.region_13.14_spmd, body=%wide.region_10.13_spmd.sunk | while | flops 138418288 | bytes 3319143 | solution.py:120
  184.6 3.8 %gather_fusion.4 = bf16[16,256,64]{2,1,0:T(8,128)(2,1)} fusion(bf16[64,256,64]{2,1,0:T(8,128)(2,1)} %get-tuple-element.642, s32[1024]{0:T(1024)S(1)} %pad_clamp_fusion.15), kind=kCustom, calls=%fused_computation.6.clone.1 | custom fusion | bytes 1048640 | tf_op jit(solution)/shard_map/while/body/gather | solution.py:34
  189.0 2.3 exponential_reduce_fusion.5
  193.6 3.8 %gather_fusion.4 = bf16[16,256,64]{2,1,0:T(8,128)(2,1)} fusion(bf16[64,256,64]{2,1,0:T(8,128)(2,1)} %get-tuple-element.642, s32[1024]{0:T(1024)S(1)} %pad_clamp_fusion.15), kind=kCustom, calls=%fused_computation.6.clone.1 | custom fusion | bytes 1048640 | tf_op jit(solution)/shard_map/while/body/gather | solution.py:34
  202.6 3.8 %gather_fusion.4 = bf16[16,256,64]{2,1,0:T(8,128)(2,1)} fusion(bf16[64,256,64]{2,1,0:T(8,128)(2,1)} %get-tuple-element.642, s32[1024]{0:T(1024)S(1)} %pad_clamp_fusion.15), kind=kCustom, calls=%fused_computation.6.clone.1 | custom fusion | bytes 1048640 | tf_op jit(solution)/shard_map/while/body/gather | solution.py:34
  211.6 3.8 %gather_fusion.4 = bf16[16,256,64]{2,1,0:T(8,128)(2,1)} fusion(bf16[64,256,64]{2,1,0:T(8,128)(2,1)} %get-tuple-element.642, s32[1024]{0:T(1024)S(1)} %pad_clamp_fusion.15), kind=kCustom, calls=%fused_computation.6.clone.1 | custom fusion | bytes 1048640 | tf_op jit(solution)/shard_map/while/body/gather | solution.py:34
  220.6 3.8 %gather_fusion.4 = bf16[16,256,64]{2,1,0:T(8,128)(2,1)} fusion(bf16[64,256,64]{2,1,0:T(8,128)(2,1)} %get-tuple-element.642, s32[1024]{0:T(1024)S(1)} %pad_clamp_fusion.15), kind=kCustom, calls=%fused_computation.6.clone.1 | custom fusion | bytes 1048640 | tf_op jit(solution)/shard_map/while/body/gather | solution.py:34
  229.7 3.8 %gather_fusion.4 = bf16[16,256,64]{2,1,0:T(8,128)(2,1)} fusion(bf16[64,256,64]{2,1,0:T(8,128)(2,1)} %get-tuple-element.642, s32[1024]{0:T(1024)S(1)} %pad_clamp_fusion.15), kind=kCustom, calls=%fused_computation.6.clone.1 | custom fusion | bytes 1048640 | tf_op jit(solution)/shard_map/while/body/gather | solution.py:34
  238.7 3.8 %gather_fusion.4 = bf16[16,256,64]{2,1,0:T(8,128)(2,1)} fusion(bf16[64,256,64]{2,1,0:T(8,128)(2,1)} %get-tuple-element.642, s32[1024]{0:T(1024)S(1)} %pad_clamp_fusion.15), kind=kCustom, calls=%fused_computation.6.clone.1 | custom fusion | bytes 1048640 | tf_op jit(solution)/shard_map/while/body/gather | solution.py:34
  247.7 3.8 %gather_fusion.4 = bf16[16,256,64]{2,1,0:T(8,128)(2,1)} fusion(bf16[64,256,64]{2,1,0:T(8,128)(2,1)} %get-tuple-element.642, s32[1024]{0:T(1024)S(1)} %pad_clamp_fusion.15), kind=kCustom, calls=%fused_computation.6.clone.1 | custom fusion | bytes 1048640 | tf_op jit(solution)/shard_map/while/body/gather | solution.py:34
  256.7 3.8 %gather_fusion.4 = bf16[16,256,64]{2,1,0:T(8,128)(2,1)} fusion(bf16[64,256,64]{2,1,0:T(8,128)(2,1)} %get-tuple-element.642, s32[1024]{0:T(1024)S(1)} %pad_clamp_fusion.15), kind=kCustom, calls=%fused_computation.6.clone.1 | custom fusion | bytes 1048640 | tf_op jit(solution)/shard_map/while/body/gather | solution.py:34
  265.7 3.8 %gather_fusion.4 = bf16[16,256,64]{2,1,0:T(8,128)(2,1)} fusion(bf16[64,256,64]{2,1,0:T(8,128)(2,1)} %get-tuple-element.642, s32[1024]{0:T(1024)S(1)} %pad_clamp_fusion.15), kind=kCustom, calls=%fused_computation.6.clone.1 | custom fusion | bytes 1048640 | tf_op jit(solution)/shard_map/while/body/gather | solution.py:34
  273.3 10.3 %all-reduce = f32[8192]{0:T(1024)S(1)} all-reduce(f32[8192]{0:T(1024)S(1)} %bitcast.147), channel_id=2, replica_groups=mesh['src'=8,'tgt'=4] {'tgt'}, use_global_device_ids=true, to_apply=%region_14.15.clone | all-reduce | flops 8192 | bytes 65536
  284.2 6.0 %all-reduce.2 = (f32[8]{0:T(128)S(1)}, f32[8,8]{1,0:T(8,128)S(1)}, f32[8,8]{1,0:T(8,128)S(1)}, f32[8]{0:T(128)S(1)}) all-reduce(f32[8]{0:T(128)S(1)} %convolution_bitcast_fusion.2, f32[8,8]{1,0:T(8,128)S(1)} %fusion.29, f32[8,8]{1,0:T(8,128)S(1)} %fusion.30, ...), channel_id=1, replica_groups=mesh['src'=8,'tgt'=4] {'tgt'}, use_global_device_ids=true, to_apply=%region_19.20 | all-reduce | flops 144 | bytes 1152 | tf_op jit(solution)/shard_map/psum | solution.py:12
  290.2 17.6 %all-reduce.1 = (f32[8]{0:T(128)S(1)}, f32[8,8]{1,0:T(8,128)S(1)}, f32[8,8]{1,0:T(8,128)S(1)}, f32[8]{0:T(128)S(1)}) all-reduce(f32[8]{0:T(128)S(1)} %get-tuple-element.297, f32[8,8]{1,0:T(8,128)S(1)} %get-tuple-element.298, f32[8,8]{1,0:T(8,128)S(1)} %get-tuple-element.299, ...), channel_id=1, replica_groups=mesh['src'=8,'tgt'=4] {'src'}, use_global_device_ids=true, to_apply=%region_20.21 | all-reduce | flops 144 | bytes 1152 | tf_op jit(solution)/shard_map/psum | solution.py:13
  (333 shorter events, 120.2 us)
Async XLA Ops:
  7.2 19.2 %copy-start = (f32[8,2048]{1,0:T(8,128)S(1)}, f32[8,2048]{1,0:T(8,128)}, u32[]{:S(2)}) copy-start(f32[8,2048]{1,0:T(8,128)} %param.19) | copy-start | bytes 196612
  7.2 8.7 %copy-start.5 = (f32[8192]{0:T(1024)S(1)}, f32[8192]{0:T(1024)}, u32[]{:S(2)}) copy-start(f32[8192]{0:T(1024)} %param.15) | copy-start | bytes 98308
  7.2 23.4 %all-gather.4.cloned.1.call-start = ((), (), s32[]{:S(2)}) async-start(), calls=%async_computation | async-start | bytes 1310720 | tf_op jit(solution)/shard_map/all_gather | solution.py:60
  11.0 12.8 %copy-start.6 = (u32[32]{0:T(128)S(1)}, u32[32]{0:T(128)}, u32[]{:S(2)}) copy-start(u32[32]{0:T(128)} %constant.169) | copy-start | bytes 388
  11.0 15.5 %copy-start.3 = (f32[8,2048]{1,0:T(8,128)S(1)}, f32[8,2048]{1,0:T(8,128)}, u32[]{:S(2)}) copy-start(f32[8,2048]{1,0:T(8,128)} %param.18) | copy-start | bytes 196612
  32.7 1.5 copy-start.1
  38.5 2.6 copy-start.2
  41.1 1.5 copy-start.1
  46.9 2.6 copy-start.2
  49.5 1.5 copy-start.1
  55.3 2.6 copy-start.2
  57.9 1.5 copy-start.1
  63.7 2.6 copy-start.2
  66.3 1.5 copy-start.1
  72.1 2.6 copy-start.2
  74.7 1.5 copy-start.1
  80.5 2.6 copy-start.2
  83.2 1.5 copy-start.1
  88.9 2.6 copy-start.2
  91.6 1.5 copy-start.1
  97.3 2.6 copy-start.2
  100.0 1.5 copy-start.1
  105.7 2.6 copy-start.2
  108.4 1.5 copy-start.1
  114.2 2.6 copy-start.2
  283.6 86.6 %copy-start.4 = (f32[2048]{0:T(1024)}, f32[2048]{0:T(1024)S(1)}, u32[]{:S(2)}) copy-start(f32[2048]{0:T(1024)S(1)} %dynamic-slice_subtract_fusion) | copy-start | bytes 24580
Sparse Core Ops, SparseCore 0:
  9.6 21.0 all-gather.3
